TPU v7x, 32 devices: a whole 2x2x4 slice. The times are simulated.
32 devices in a mesh: rep: 8 (over y, x, core), tp: 4 (over z).
Axes of the slice: x: 2, y: 2, z: 4, core: 2. Of those that a mesh axis runs over, the one named last changes fastest.
Arguments:
- queries: bfloat16 [2048, 4096], P('rep', 'tp'), may hold values from -120 to 120
- keys_new: bfloat16 [2048, 1024], P('rep', 'tp'), may hold values from -7 to 7
- values_new: bfloat16 [2048, 1024], P('rep', 'tp'), may hold values from -6 to 6
- caches: bfloat16 [16, 2, 4096, 1024], P('rep', None, None, 'tp'), may hold values from -6 to 6
- lengths: int32 [8, 2], replicated, may hold values from 128 to 4096, as said below
- moving: int32 [8], replicated, may hold values from 0 to 1
- destination: int32 [8], replicated, may hold values from 0 to 7, each once
- out_weight: bfloat16 [4096, 4096], P('tp'), may hold values from -0.09375 to 0.09375
Outputs:
- mixed: bfloat16 [2048, 4096], P('rep', 'tp')
- held_cache: bfloat16 [16, 2, 4096, 1024], P('rep', None, None, 'tp')
Inputs may be any that keep to these rules, and one draw needn't show every extreme that they name: `lengths`: multiples of 128; in every draw some slot holds 4096 and some 128. `destination`: each replica receives exactly one failing candidate; it takes the slot that its own failing candidate leaves.
All inputs are finite; a program needn't handle non-finite values.
Results may differ from a plain program's by a relative error of at most 0.014.
Values may be sent and summed in bfloat16 or wider, within the bound.
A program may use at most 64 MiB of HBM per device.

v0:
```python
import jax
import jax.numpy as jnp
from jax import lax
from jax.sharding import PartitionSpec as P

HEAD = 128
masked_score = -1e30
key_block_rows = 512


def attend(query_slot, key_cache, value_cache, length, keys_fresh, values_fresh, block_count):
    span_rows = query_slot.shape[0]
    kv_count = key_cache.shape[1] // HEAD
    group_size = query_slot.shape[1] // (HEAD * kv_count)
    grouped = query_slot.reshape(span_rows, kv_count, group_size, HEAD).transpose(1, 2, 0, 3)
    grouped = grouped.reshape(kv_count, group_size * span_rows, HEAD)
    scale = HEAD ** (-0.5)
    token_of_row = jnp.arange(group_size * span_rows, dtype=jnp.int32) % span_rows

    def absorb(running, key_block, value_block, visible):
        row_max, row_total, weighted = running
        scores = (
            jnp.einsum("gqd,kgd->gqk", grouped, key_block, preferred_element_type=jnp.float32)
            * scale
        )
        scores = jnp.where(visible, scores, masked_score)
        new_max = jnp.maximum(row_max, jnp.max(scores, axis=2))
        rescale = jnp.exp(row_max - new_max)
        weights_block = jnp.where(visible, jnp.exp(scores - new_max[:, :, None]), 0.0)
        row_total = row_total * rescale + jnp.sum(weights_block, axis=2)
        weighted = weighted * rescale[:, :, None] + jnp.einsum(
            "gqk,kgd->gqd",
            weights_block.astype(jnp.bfloat16),
            value_block,
            preferred_element_type=jnp.float32,
        )
        return (new_max, row_total, weighted)

    def cache_step(block_index, running):
        start = block_index * key_block_rows
        key_block = lax.dynamic_slice_in_dim(key_cache, start, key_block_rows, 0).reshape(
            key_block_rows, kv_count, HEAD
        )
        value_block = lax.dynamic_slice_in_dim(value_cache, start, key_block_rows, 0).reshape(
            key_block_rows, kv_count, HEAD
        )
        visible = (start + jnp.arange(key_block_rows, dtype=jnp.int32) < length)[None, None, :]
        return absorb(running, key_block, value_block, visible)

    rows_all = group_size * span_rows
    initial = (
        jnp.full((kv_count, rows_all), masked_score, jnp.float32),
        jnp.zeros((kv_count, rows_all), jnp.float32),
        jnp.zeros((kv_count, rows_all, HEAD), jnp.float32),
    )
    running = lax.fori_loop(0, block_count, cache_step, initial)
    visible = (jnp.arange(span_rows, dtype=jnp.int32)[None, :] <= token_of_row[:, None])[None]
    running = absorb(
        running,
        keys_fresh.reshape(span_rows, kv_count, HEAD),
        values_fresh.reshape(span_rows, kv_count, HEAD),
        visible,
    )
    result = running[2] / running[1][:, :, None]
    result = result.reshape(kv_count, group_size, span_rows, HEAD).transpose(2, 0, 1, 3)
    return result.reshape(span_rows, kv_count * group_size * HEAD).astype(jnp.bfloat16)


def on_device(queries, keys_new, values_new, caches, lengths, moving, destination, out_weight):
    replicas = lax.axis_size("rep")
    own_index = lax.axis_index("rep")
    slot_count = caches.shape[0]
    cache_rows = caches.shape[2]
    width_local = caches.shape[3]
    piece_rows = cache_rows // replicas
    leaving_slot = moving[own_index]
    leaving = lax.dynamic_index_in_dim(caches, leaving_slot, 0, keepdims=False)
    spread = lax.all_to_all(leaving, "rep", split_axis=1, concat_axis=1, tiled=True)
    source_of = jnp.argsort(destination)
    gathered_pieces = spread.reshape(2, replicas, piece_rows, width_local)
    ordered = jnp.take(gathered_pieces, source_of, axis=1).reshape(2, cache_rows, width_local)
    arrived = lax.all_to_all(ordered, "rep", split_axis=1, concat_axis=1, tiled=True)
    anchor = source_of[own_index]
    incoming_length = lengths[anchor, moving[anchor]]
    updated = lax.dynamic_update_index_in_dim(caches, arrived, leaving_slot, 0)
    own_lengths = lengths[own_index]
    held_lengths = jnp.where(jnp.arange(slot_count) == leaving_slot, incoming_length, own_lengths)
    span_rows = queries.shape[0] // slot_count
    results = []
    for slot_number in range(slot_count):
        length = held_lengths[slot_number]
        block_count = cache_rows // key_block_rows
        lower = slot_number * span_rows
        results.append(
            attend(
                queries[lower : lower + span_rows],
                updated[slot_number, 0],
                updated[slot_number, 1],
                length,
                keys_new[lower : lower + span_rows],
                values_new[lower : lower + span_rows],
                block_count,
            )
        )
    attended = jnp.concatenate(results, axis=0)
    partial_value = jnp.dot(attended, out_weight, preferred_element_type=jnp.float32)
    mixed = lax.psum_scatter(
        partial_value.astype(jnp.bfloat16), "tp", scatter_dimension=1, tiled=True
    )
    return (mixed, updated)


def solution(mesh):
    in_specs = (
        P("rep", "tp"),
        P("rep", "tp"),
        P("rep", "tp"),
        P("rep", None, None, "tp"),
        P(),
        P(),
        P(),
        P("tp", None),
    )
    out_specs = (P("rep", "tp"), P("rep", None, None, "tp"))
    return jax.shard_map(
        on_device, mesh=mesh, in_specs=in_specs, out_specs=out_specs, check_vma=False
    )
```

profile of v0, /device:TPU:0, one launch (start us, length us, event | category | flops | bytes accessed | tf_op | source)
XLA Modules:
  0.0 365.8 jit_solution(7094466064213119870)
XLA Ops:
  7.2 7.3 %copy.152 = bf16[2,2,4096,256]{3,2,1,0:T(8,128)(2,1)} copy(bf16[2,2,4096,256]{3,2,1,0:T(8,128)(2,1)} %param.15) | data formatting | bytes 16777216
  20.5 2.5 constant_dynamic-slice_fusion.4
  23.0 27.2 %copy.117 = bf16[1,2,4096,256]{3,1,2,0:T(2,128)(2,1)} copy(bf16[1,2,4096,256]{3,2,1,0:T(8,128)(2,1)S(1)} %constant_dynamic-slice_fusion.4) | data formatting | bytes 8388608 | tf_op jit(solution)/shard_map/jit(dynamic_index_in_dim)/dynamic_slice | solution.py:77
  50.2 5.2 %all-to-all-start = ((bf16[2,4096,256]{2,0,1:T(2,128)(2,1)}), bf16[2,4096,256]{2,0,1:T(2,128)(2,1)}, u32[]{:S(2)}, u32[]{:S(2)}) async-start(bf16[2,4096,256]{2,0,1:T(2,128)(2,1)} %bitcast.118), calls=%async_computation | async-start | bytes 8388608 | tf_op jit(solution)/shard_map/all_to_all | solution.py:78
  55.5 49.1 %all-to-all-done = bf16[2,4096,256]{2,0,1:T(2,128)(2,1)} async-done(((bf16[2,4096,256]{2,0,1:T(2,128)(2,1)}), bf16[2,4096,256]{2,0,1:T(2,128)(2,1)}, u32[]{:S(2)}, u32[]{:S(2)}) %all-to-all-start) | async-done | bytes 4194336 | tf_op jit(solution)/shard_map/all_to_all | solution.py:78
  104.5 4.7 %copy.72 = bf16[2,4096,256]{2,1,0:T(8,128)(2,1)} copy(bf16[2,4096,256]{2,0,1:T(2,128)(2,1)} %all-to-all-done) | data formatting | bytes 8388608 | tf_op jit(solution)/shard_map/all_to_all | solution.py:78
  109.2 4.9 %gather_fusion = bf16[8,2,512,256]{3,2,1,0:T(8,128)(2,1)} fusion(bf16[2,8,512,256]{3,2,1,0:T(8,128)(2,1)} %bitcast.119, s32[1024]{0:T(1024)S(1)} %pad_clamp_fusion), kind=kCustom, calls=%fused_computation | custom fusion | bytes 8388640 | tf_op jit(solution)/shard_map/jit(_take)/gather | solution.py:81
  114.2 2.5 copy.73
  117.7 27.2 %copy.74 = bf16[2,4096,256]{2,0,1:T(2,128)(2,1)} copy(bf16[2,4096,256]{2,1,0:T(8,128)(2,1)S(1)} %bitcast_select_fusion) | data formatting | bytes 8388608 | tf_op jit(solution)/shard_map/jit(_take)/select_n | solution.py:81
  144.9 4.7 %all-to-all-start.1 = ((bf16[2,4096,256]{2,0,1:T(2,128)(2,1)}), bf16[2,4096,256]{2,0,1:T(2,128)(2,1)}, u32[]{:S(2)}, u32[]{:S(2)}) async-start(bf16[2,4096,256]{2,0,1:T(2,128)(2,1)} %copy.74), calls=%async_computation.1 | async-start | bytes 8388608 | tf_op jit(solution)/shard_map/all_to_all | solution.py:82
  154.8 1.2 compare_select_fusion.1
  156.7 1.1 fusion.62
  157.8 1.1 fusion.63
  159.0 39.7 %all-to-all-done.1 = bf16[2,4096,256]{2,0,1:T(2,128)(2,1)} async-done(((bf16[2,4096,256]{2,0,1:T(2,128)(2,1)}), bf16[2,4096,256]{2,0,1:T(2,128)(2,1)}, u32[]{:S(2)}, u32[]{:S(2)}) %all-to-all-start.1) | async-done | bytes 4194336 | tf_op jit(solution)/shard_map/all_to_all | solution.py:82
  198.6 4.7 %copy_dynamic-update-slice_fusion = bf16[2,2,4096,256]{3,2,1,0:T(8,128)(2,1)} fusion(bf16[2,2,4096,256]{3,2,1,0:T(8,128)(2,1)} %copy.152, s32[]{:T(128)S(6)} %select_n.120, bf16[1,2,4096,256]{3,1,2,0:T(2,128)(2,1)} %bitcast.9), kind=kLoop, calls=%fused_computation.53 | loop fusion | bytes 8388612 | tf_op jit(solution)/shard_map/jit(dynamic_update_index_in_dim)/dynamic_update_slice | solution.py:85
  203.4 5.9 %slice_bitcast_fusion.2 = (bf16[4096,256]{1,0:T(8,128)(2,1)}, bf16[4096,256]{1,0:T(8,128)(2,1)}, bf16[4096,256]{1,0:T(8,128)(2,1)}, bf16[4096,256]{1,0:T(8,128)(2,1)}) fusion(bf16[2,2,4096,256]{3,2,1,0:T(8,128)(2,1)} %copy_dynamic-update-slice_fusion), kind=kLoop, calls=%fused_computation.57 | loop fusion | bytes 16777216 | tf_op jit(solution)/shard_map/squeeze | solution.py:98
  209.3 47.3 %while.36 = (s32[]{:T(128)}, f32[2,512]{1,0:T(2,128)S(1)}, f32[2,512]{1,0:T(2,128)S(1)}, f32[2,512,128]{2,1,0:T(8,128)}, s32[]{:T(128)}, /*index=5*/bf16[4096,25...) while((s32[]{:T(128)}, f32[2,512]{1,0:T(2,128)S(1)}, ...), condition=%wide.region_4.5_spmd.clone, body=%wide.region_1.4_spmd.clone.sunk | while | flops 275650560 | bytes 10291387 | solution.py:56
  209.3 1.1 constant_dynamic-slice_fusion.7
  212.5 1.8 convolution_add_fusion.6
  214.3 1.1 constant_dynamic-slice_fusion.7
  217.5 2.8 convolution_add_fusion.6
  220.4 1.1 constant_dynamic-slice_fusion.7
  223.6 2.8 convolution_add_fusion.6
  226.4 1.1 constant_dynamic-slice_fusion.7
  229.6 2.8 convolution_add_fusion.6
  232.5 1.1 constant_dynamic-slice_fusion.7
  235.7 2.8 convolution_add_fusion.6
  238.5 1.1 constant_dynamic-slice_fusion.7
  241.7 2.8 convolution_add_fusion.6
  244.6 1.1 constant_dynamic-slice_fusion.7
  247.8 2.8 convolution_add_fusion.6
  250.6 1.1 constant_dynamic-slice_fusion.7
  253.8 2.8 convolution_add_fusion.6
  256.7 47.2 %while.37 = (s32[]{:T(128)}, f32[2,512]{1,0:T(2,128)S(1)}, f32[2,512]{1,0:T(2,128)S(1)}, f32[2,512,128]{2,1,0:T(8,128)}, s32[]{:T(128)}, /*index=5*/bf16[4096,25...) while((s32[]{:T(128)}, f32[2,512]{1,0:T(2,128)S(1)}, ...), condition=%wide.region_10.11_spmd.clone, body=%wide.region_7.10_spmd.clone.sunk | while | flops 275650560 | bytes 10291387 | solution.py:56
  256.7 1.1 constant_dynamic-slice_fusion.8
  259.9 1.8 convolution_add_fusion.7
  264.9 2.8 convolution_add_fusion.7
  270.9 2.8 convolution_add_fusion.7
  273.8 1.1 constant_dynamic-slice_fusion.8
  277.0 2.8 convolution_add_fusion.7
  283.0 2.8 convolution_add_fusion.7
  289.0 2.8 convolution_add_fusion.7
  295.0 2.8 convolution_add_fusion.7
  301.1 2.8 convolution_add_fusion.7
  304.0 1.3 fusion.39
  305.3 1.7 fusion.34
  308.0 7.1 %convolution_convert_fusion = bf16[256,4096]{1,0:T(8,128)(2,1)} fusion(bf16[1024,4096]{1,0:T(8,128)(2,1)} %param.19, bf16[128,1024]{0,1:T(8,128)(2,1)S(1)} %bitcast.128, bf16[128,1024]{0,1:T(8,128)(2,1)S(1)} %bitcast.127), kind=kOutput, calls=%fused_computation.51 | convolution fusion | flops 2149580800 | bytes 11010048 | tf_op jit(solution)/shard_map/dot_general | solution.py:106
  315.1 43.9 %reduce-scatter.2.cloned.1.call-done = bf16[256,1024]{1,0:T(8,128)(2,1)} async-done(((bf16[256,4096]{1,0:T(8,128)(2,1)}), bf16[256,1024]{1,0:T(8,128)(2,1)}) %reduce-scatter.2.cloned.1.call-update) | async-done | bytes 524304 | tf_op jit(solution)/shard_map/reduce_scatter | solution.py:107
  (192 shorter events, 47.8 us)
Async XLA Ops:
  7.2 10.8 %copy-start.6 = (s32[8]{0:T(128)S(1)}, s32[8]{0:T(128)}, u32[]{:S(2)}) copy-start(s32[8]{0:T(128)} %param.17) | copy-start | bytes 100
  7.2 7.3 %copy-start.7 = (s32[8]{0:T(128)S(1)}, s32[8]{0:T(128)}, u32[]{:S(2)}) copy-start(s32[8]{0:T(128)} %param.18) | copy-start | bytes 100
  50.2 54.4 %all-to-all-start = ((bf16[2,4096,256]{2,0,1:T(2,128)(2,1)}), bf16[2,4096,256]{2,0,1:T(2,128)(2,1)}, u32[]{:S(2)}, u32[]{:S(2)}) async-start(bf16[2,4096,256]{2,0,1:T(2,128)(2,1)} %bitcast.118), calls=%async_computation | async-start | bytes 8388608 | tf_op jit(solution)/shard_map/all_to_all | solution.py:78
  144.9 6.3 %copy-start.5 = (s32[8,2]{0,1:T(2,128)S(1)}, s32[8,2]{0,1:T(2,128)}, u32[]{:S(2)}) copy-start(s32[8,2]{0,1:T(2,128)} %param.16) | copy-start | bytes 196
  144.9 7.7 %copy-start.1 = (bf16[256,1024]{1,0:T(8,128)(2,1)S(1)}, bf16[256,1024]{1,0:T(8,128)(2,1)}, u32[]{:S(2)}) copy-start(bf16[256,1024]{1,0:T(8,128)(2,1)} %param.12) | copy-start | bytes 1572868
  144.9 53.8 %all-to-all-start.1 = ((bf16[2,4096,256]{2,0,1:T(2,128)(2,1)}), bf16[2,4096,256]{2,0,1:T(2,128)(2,1)}, u32[]{:S(2)}, u32[]{:S(2)}) async-start(bf16[2,4096,256]{2,0,1:T(2,128)(2,1)} %copy.74), calls=%async_computation.1 | async-start | bytes 8388608 | tf_op jit(solution)/shard_map/all_to_all | solution.py:82
  149.5 3.3 copy-start.2
  149.6 3.8 %copy-start.3 = (bf16[256,256]{1,0:T(8,128)(2,1)S(1)}, bf16[256,256]{1,0:T(8,128)(2,1)}, u32[]{:S(2)}) copy-start(bf16[256,256]{1,0:T(8,128)(2,1)} %param.14) | copy-start | bytes 393220
  149.6 209.4 %reduce-scatter.2.cloned.1.call-start = ((), (), s32[]{:S(2)}) async-start(), calls=%async_computation.3 | async-start | bytes 2621440 | tf_op jit(solution)/shard_map/reduce_scatter | solution.py:107
  256.7 47.3 %copy-start = (f32[2,512,128]{1,2,0:T(8,128)S(1)}, f32[2,512,128]{1,2,0:T(8,128)}, u32[]{:S(2)}) copy-start(f32[2,512,128]{1,2,0:T(8,128)} %get-tuple-element.461) | copy-start | bytes 1572868
  303.9 3.3 copy-start.4
  303.9 3.3 copy-start.8
Sparse Core Ops, SparseCore 0:
  315.2 43.7 reduce-scatter.1
where the time goes:
time: 368 us; the launch traced here: 366 us
  waiting for transfers between devices  133 us (36%)
  local copies, waits for them, and re-layouts  114 us (31%)
  matrix products  63.8 us (17%)
  other arithmetic  24.7 us (7%)
  between operations  20.1 us (5%)
  starting transfers between devices  10.1 us (3%)
    all_to_all x1, waiting for transfers between devices, on_device(): lax.all_to_all(leaving, 'rep', split_axis=1, concat_axis=1, tiled=True)  49.1 us
    dot_general x18, matrix products, absorb(): jnp.einsum('gqk,kgd->gqd', weights_block.astype(jnp.bfloat16), value_bloc...  45.6 us
    reduce_scatter x1, waiting for transfers between devices, on_device(): lax.psum_scatter(partial_value.astype(jnp.bfloat16), 'tp', scatter_dimens...  43.9 us
    all_to_all x1, waiting for transfers between devices, on_device(): lax.all_to_all(ordered, 'rep', split_axis=1, concat_axis=1, tiled=True)  39.7 us
    dynamic_slice x2, local copies, waits for them, and re-layouts, on_device(): leaving = lax.dynamic_index_in_dim(caches, leaving_slot, 0, keepdims=False)  29.7 us
    select_n x1, local copies, waits for them, and re-layouts, on_device(): jnp.take(gathered_pieces, source_of, axis=1)  27.2 us
    dynamic_slice x32, local copies, waits for them, and re-layouts, cache_step(): lax.dynamic_slice_in_dim(value_cache, start, key_block_rows, 0)  19.3 us
    dot_general x18, matrix products, absorb(): jnp.einsum('gqd,kgd->gqk', grouped, key_block, preferred_element_type=jnp...  11.1 us
  transfers between devices with their start and end apart: 3, of which 3 were waited for; matrix products, arithmetic and copies ran while one was open for 2% of the time, Pallas kernels for 0%

commit v1 on v0

--- a/solution.py
+++ b/solution.py
@@ -79,7 +79,10 @@
     source_of = jnp.argsort(destination)
     gathered_pieces = spread.reshape(2, replicas, piece_rows, width_local)
     ordered = jnp.take(gathered_pieces, source_of, axis=1).reshape(2, cache_rows, width_local)
-    arrived = lax.all_to_all(ordered, "rep", split_axis=1, concat_axis=1, tiled=True)
+    arrived = jnp.concatenate(
+        lax.all_to_all(jnp.stack(jnp.split(ordered, lax.axis_size("rep"), axis=1)), "rep", 0, 0),
+        axis=1,
+    )
     anchor = source_of[own_index]
     incoming_length = lengths[anchor, moving[anchor]]
     updated = lax.dynamic_update_index_in_dim(caches, arrived, leaving_slot, 0)

time: 368 us -> 347 us (0.943)
  local copies, waits for them, and re-layouts: 114 us -> 93.2 us
    select_n x1 -> x0, local copies, waits for them, and re-layouts: 27.2 us -> none  [on_device(): jnp.take(gathered_pieces, source_of, axis=1)]
    unnamed x25 -> x32, local copies, waits for them, and re-layouts: 9.12 us -> 15 us
where the time goes in v1:
time: 347 us; the launch traced here: 345 us
  waiting for transfers between devices  133 us (38%)
  local copies, waits for them, and re-layouts  93.2 us (27%)
  matrix products  63.8 us (18%)
  other arithmetic  24.6 us (7%)
  between operations  19.7 us (6%)
  starting transfers between devices  10.1 us (3%)
    all_to_all x1, waiting for transfers between devices, on_device(): lax.all_to_all(leaving, 'rep', split_axis=1, concat_axis=1, tiled=True)  49.1 us
    dot_general x18, matrix products, absorb(): jnp.einsum('gqk,kgd->gqd', weights_block.astype(jnp.bfloat16), value_bloc...  45.6 us
    reduce_scatter x1, waiting for transfers between devices, on_device(): lax.psum_scatter(partial_value.astype(jnp.bfloat16), 'tp', scatter_dimens...  43.9 us
    all_to_all x1, waiting for transfers between devices, on_device(): lax.all_to_all(jnp.stack(jnp.split(ordered, lax.axis_size('rep'), axis=1)...  40 us
    dynamic_slice x2, local copies, waits for them, and re-layouts, on_device(): leaving = lax.dynamic_index_in_dim(caches, leaving_slot, 0, keepdims=False)  29.7 us
    dynamic_slice x32, local copies, waits for them, and re-layouts, cache_step(): lax.dynamic_slice_in_dim(value_cache, start, key_block_rows, 0)  19.3 us
    unnamed x32, local copies, waits for them, and re-layouts  15 us
    dot_general x18, matrix products, absorb(): jnp.einsum('gqd,kgd->gqk', grouped, key_block, preferred_element_type=jnp...  11.1 us
  transfers between devices with their start and end apart: 3, of which 3 were waited for; matrix products, arithmetic and copies ran while one was open for 2% of the time, Pallas kernels for 0%

profile of v1, /device:TPU:0, one launch (start us, length us, event | category | flops | bytes accessed | tf_op | source)
XLA Modules:
  0.0 345.2 jit_solution(17953803184644193642)
XLA Ops:
  7.2 7.3 %copy.197 = bf16[2,2,4096,256]{3,2,1,0:T(8,128)(2,1)} copy(bf16[2,2,4096,256]{3,2,1,0:T(8,128)(2,1)} %param.15) | data formatting | bytes 16777216
  20.3 2.5 constant_dynamic-slice_fusion.4
  22.8 27.2 %copy.155 = bf16[1,2,4096,256]{3,1,2,0:T(2,128)(2,1)} copy(bf16[1,2,4096,256]{3,2,1,0:T(8,128)(2,1)S(1)} %constant_dynamic-slice_fusion.4) | data formatting | bytes 8388608 | tf_op jit(solution)/shard_map/jit(dynamic_index_in_dim)/dynamic_slice | solution.py:77
  50.0 5.2 %all-to-all-start = ((bf16[2,4096,256]{2,0,1:T(2,128)(2,1)}), bf16[2,4096,256]{2,0,1:T(2,128)(2,1)}, u32[]{:S(2)}, u32[]{:S(2)}) async-start(bf16[2,4096,256]{2,0,1:T(2,128)(2,1)} %bitcast.151), calls=%async_computation | async-start | bytes 8388608 | tf_op jit(solution)/shard_map/all_to_all | solution.py:78
  55.3 49.1 %all-to-all-done = bf16[2,4096,256]{2,0,1:T(2,128)(2,1)} async-done(((bf16[2,4096,256]{2,0,1:T(2,128)(2,1)}), bf16[2,4096,256]{2,0,1:T(2,128)(2,1)}, u32[]{:S(2)}, u32[]{:S(2)}) %all-to-all-start) | async-done | bytes 4194336 | tf_op jit(solution)/shard_map/all_to_all | solution.py:78
  104.4 4.7 %copy.112 = bf16[2,4096,256]{2,1,0:T(8,128)(2,1)} copy(bf16[2,4096,256]{2,0,1:T(2,128)(2,1)} %all-to-all-done) | data formatting | bytes 8388608 | tf_op jit(solution)/shard_map/all_to_all | solution.py:78
  109.1 4.9 %gather_fusion = bf16[8,2,512,256]{3,2,1,0:T(8,128)(2,1)} fusion(bf16[2,8,512,256]{3,2,1,0:T(8,128)(2,1)} %bitcast.153, s32[1024]{0:T(1024)S(1)} %pad_clamp_fusion), kind=kCustom, calls=%fused_computation | custom fusion | bytes 8388640 | tf_op jit(solution)/shard_map/jit(_take)/gather | solution.py:81
  114.0 2.5 copy.113
  124.2 4.7 %all-to-all-start.1 = ((bf16[8,2,512,256]{3,2,1,0:T(8,128)(2,1)}), bf16[8,2,512,256]{3,2,1,0:T(8,128)(2,1)}, u32[]{:S(2)}, u32[]{:S(2)}) async-start(bf16[8,2,512,256]{3,2,1,0:T(8,128)(2,1)} %fusion.36), calls=%async_computation.1 | async-start | bytes 8388608 | tf_op jit(solution)/shard_map/all_to_all | solution.py:83
  133.8 1.2 compare_select_fusion.1
  135.7 1.1 fusion.70
  136.8 1.1 fusion.71
  137.9 40.0 %all-to-all-done.1 = bf16[8,2,512,256]{3,2,1,0:T(8,128)(2,1)} async-done(((bf16[8,2,512,256]{3,2,1,0:T(8,128)(2,1)}), bf16[8,2,512,256]{3,2,1,0:T(8,128)(2,1)}, u32[]{:S(2)}, u32[]{:S(2)}) %all-to-all-start.1) | async-done | bytes 4194336 | tf_op jit(solution)/shard_map/all_to_all | solution.py:83
  178.0 2.5 copy.114
  180.4 2.3 constant_dynamic-update-slice_fusion
  182.7 5.9 %slice_bitcast_fusion.2 = (bf16[4096,256]{1,0:T(8,128)(2,1)}, bf16[4096,256]{1,0:T(8,128)(2,1)}, bf16[4096,256]{1,0:T(8,128)(2,1)}, bf16[4096,256]{1,0:T(8,128)(2,1)}) fusion(bf16[2,2,4096,256]{3,2,1,0:T(8,128)(2,1)} %constant_dynamic-update-slice_fusion), kind=kLoop, calls=%fused_computation.56 | loop fusion | bytes 16777216 | tf_op jit(solution)/shard_map/squeeze | solution.py:101
  188.7 47.3 %while.36 = (s32[]{:T(128)}, f32[2,512]{1,0:T(2,128)S(1)}, f32[2,512]{1,0:T(2,128)S(1)}, f32[2,512,128]{2,1,0:T(8,128)}, s32[]{:T(128)}, /*index=5*/bf16[4096,25...) while((s32[]{:T(128)}, f32[2,512]{1,0:T(2,128)S(1)}, ...), condition=%wide.region_4.5_spmd.clone, body=%wide.region_1.4_spmd.clone.sunk | while | flops 275650560 | bytes 10291387 | solution.py:56
  188.7 1.1 constant_dynamic-slice_fusion.7
  191.9 1.8 convolution_add_fusion.6
  193.7 1.1 constant_dynamic-slice_fusion.7
  196.9 2.8 convolution_add_fusion.6
  199.7 1.1 constant_dynamic-slice_fusion.7
  202.9 2.8 convolution_add_fusion.6
  209.0 2.8 convolution_add_fusion.6
  211.8 1.1 constant_dynamic-slice_fusion.7
  215.0 2.8 convolution_add_fusion.6
  217.9 1.1 constant_dynamic-slice_fusion.7
  221.1 2.8 convolution_add_fusion.6
  227.1 2.8 convolution_add_fusion.6
  230.0 1.1 constant_dynamic-slice_fusion.7
  233.2 2.8 convolution_add_fusion.6
  236.0 47.2 %while.37 = (s32[]{:T(128)}, f32[2,512]{1,0:T(2,128)S(1)}, f32[2,512]{1,0:T(2,128)S(1)}, f32[2,512,128]{2,1,0:T(8,128)}, s32[]{:T(128)}, /*index=5*/bf16[4096,25...) while((s32[]{:T(128)}, f32[2,512]{1,0:T(2,128)S(1)}, ...), condition=%wide.region_10.11_spmd.clone, body=%wide.region_7.10_spmd.clone.sunk | while | flops 275650560 | bytes 10291387 | solution.py:56
  236.0 1.1 constant_dynamic-slice_fusion.8
  239.3 1.8 convolution_add_fusion.7
  241.1 1.1 constant_dynamic-slice_fusion.8
  244.2 2.8 convolution_add_fusion.7
  247.1 1.1 constant_dynamic-slice_fusion.8
  250.3 2.8 convolution_add_fusion.7
  253.1 1.1 constant_dynamic-slice_fusion.8
  256.3 2.8 convolution_add_fusion.7
  262.3 2.8 convolution_add_fusion.7
  268.4 2.8 convolution_add_fusion.7
  274.4 2.8 convolution_add_fusion.7
  280.4 2.8 convolution_add_fusion.7
  283.3 1.3 fusion.47
  284.6 1.7 fusion.34
  287.3 7.1 %convolution_convert_fusion = bf16[256,4096]{1,0:T(8,128)(2,1)} fusion(bf16[1024,4096]{1,0:T(8,128)(2,1)} %param.19, bf16[128,1024]{0,1:T(8,128)(2,1)S(1)} %bitcast.162, bf16[128,1024]{0,1:T(8,128)(2,1)S(1)} %bitcast.161), kind=kOutput, calls=%fused_computation.51 | convolution fusion | flops 2149580800 | bytes 11010048 | tf_op jit(solution)/shard_map/dot_general | solution.py:109
  294.4 43.9 %reduce-scatter.2.cloned.1.call-done = bf16[256,1024]{1,0:T(8,128)(2,1)} async-done(((bf16[256,4096]{1,0:T(8,128)(2,1)}), bf16[256,1024]{1,0:T(8,128)(2,1)}) %reduce-scatter.2.cloned.1.call-update) | async-done | bytes 524304 | tf_op jit(solution)/shard_map/reduce_scatter | solution.py:110
  (200 shorter events, 54.5 us)
Async XLA Ops:
  7.2 10.8 %copy-start.6 = (s32[8]{0:T(128)S(1)}, s32[8]{0:T(128)}, u32[]{:S(2)}) copy-start(s32[8]{0:T(128)} %param.17) | copy-start | bytes 100
  7.2 7.3 %copy-start.7 = (s32[8]{0:T(128)S(1)}, s32[8]{0:T(128)}, u32[]{:S(2)}) copy-start(s32[8]{0:T(128)} %param.18) | copy-start | bytes 100
  50.0 54.4 %all-to-all-start = ((bf16[2,4096,256]{2,0,1:T(2,128)(2,1)}), bf16[2,4096,256]{2,0,1:T(2,128)(2,1)}, u32[]{:S(2)}, u32[]{:S(2)}) async-start(bf16[2,4096,256]{2,0,1:T(2,128)(2,1)} %bitcast.151), calls=%async_computation | async-start | bytes 8388608 | tf_op jit(solution)/shard_map/all_to_all | solution.py:78
  124.2 6.1 %copy-start.5 = (s32[8,2]{0,1:T(2,128)S(1)}, s32[8,2]{0,1:T(2,128)}, u32[]{:S(2)}) copy-start(s32[8,2]{0,1:T(2,128)} %param.16) | copy-start | bytes 196
  124.2 7.4 %copy-start.1 = (bf16[256,1024]{1,0:T(8,128)(2,1)S(1)}, bf16[256,1024]{1,0:T(8,128)(2,1)}, u32[]{:S(2)}) copy-start(bf16[256,1024]{1,0:T(8,128)(2,1)} %param.12) | copy-start | bytes 1572868
  124.2 53.8 %all-to-all-start.1 = ((bf16[8,2,512,256]{3,2,1,0:T(8,128)(2,1)}), bf16[8,2,512,256]{3,2,1,0:T(8,128)(2,1)}, u32[]{:S(2)}, u32[]{:S(2)}) async-start(bf16[8,2,512,256]{3,2,1,0:T(8,128)(2,1)} %fusion.36), calls=%async_computation.1 | async-start | bytes 8388608 | tf_op jit(solution)/shard_map/all_to_all | solution.py:83
  128.9 3.0 copy-start.2
  128.9 3.5 %copy-start.3 = (bf16[256,256]{1,0:T(8,128)(2,1)S(1)}, bf16[256,256]{1,0:T(8,128)(2,1)}, u32[]{:S(2)}) copy-start(bf16[256,256]{1,0:T(8,128)(2,1)} %param.14) | copy-start | bytes 393220
  128.9 209.4 %reduce-scatter.2.cloned.1.call-start = ((), (), s32[]{:S(2)}) async-start(), calls=%async_computation.3 | async-start | bytes 2621440 | tf_op jit(solution)/shard_map/reduce_scatter | solution.py:110
  236.0 47.3 %copy-start = (f32[2,512,128]{1,2,0:T(8,128)S(1)}, f32[2,512,128]{1,2,0:T(8,128)}, u32[]{:S(2)}) copy-start(f32[2,512,128]{1,2,0:T(8,128)} %get-tuple-element.477) | copy-start | bytes 1572868
  283.3 3.3 copy-start.4
  283.3 3.3 copy-start.8
Sparse Core Ops, SparseCore 0:
  294.6 43.7 reduce-scatter.1
